TPU v7x, 32 devices: a whole 2x2x4 slice. The times are simulated.
32 devices in a mesh: seq: 16 (over z, y, x), fsdp: 2 (over core).
Axes of the slice: x: 2, y: 2, z: 4, core: 2. Of those that a mesh axis runs over, the one named last changes fastest.
Arguments:
- tokens: bfloat16 [2, 12288, 2560], P('fsdp', 'seq'), may hold values from -6 to 6
- bounds: int32 [2, 16, 2], P('fsdp', 'seq'), may hold values from 0 to 24, as said below
- in_weight: bfloat16 [2560, 5416], P(('seq', 'fsdp')), may hold values from -0.125 to 0.125
- conv_weight: float32 [4, 2816], replicated, may hold values from -0.6 to 0.6
- conv_bias: float32 [2816], replicated, may hold values from -3 to 3
- dt_bias: float32 [40], replicated, may hold values from -4 to 0
- decay_rate: float32 [40], replicated, may hold values from 4.8828125e-05 to 0.5
- skip_gain: float32 [40], replicated, may hold values from 0.1 to 1.9
- norm_gain: float32 [2560], replicated, may hold values from 0.1 to 1.9
Outputs:
- layer_out: bfloat16 [2, 12288, 2560], P('fsdp', 'seq')
Inputs may be any that keep to these rules, and one draw needn't show every extreme that they name: For sequence b, bounds[b, s] holds the first and one past the last block of the shard of index s of seq; shards are consecutive in s and cover all 24 blocks; each holds 1 to 3 blocks, and some shard holds 3.
All inputs are finite; a program needn't handle non-finite values.
Results may differ from a plain program's by a relative error of at most 0.0028.
The roundings to bfloat16 on the way count: a program that leaves them out, or rounds other values in their place, can miss the bound.
Values may be sent and summed in bfloat16 or wider, within the bound.
A program may use at most 192 MiB of HBM per device.

v0:
```python
import jax
import jax.numpy as jnp
from jax import lax
from jax.sharding import PartitionSpec as P

BLOCK = 256


def passed_along(value, axis, steps):
    count = lax.axis_size(axis)
    leading, last = (max(0, -steps), min(count, count - steps))
    return lax.ppermute(value, axis, [(source, source + steps) for source in range(leading, last)])


def carried_in(part, axis, combine, identity):
    place = lax.axis_index(axis)
    gathered = jax.tree.map(lambda a: lax.all_gather(a, axis), part)
    state = jax.tree.map(lambda a, e: jnp.zeros_like(a) + jnp.asarray(e, a.dtype), part, identity)

    def one(turn, state):
        return combine(
            state, jax.tree.map(lambda a: lax.dynamic_index_in_dim(a, turn, 0, False), gathered)
        )

    return lax.fori_loop(0, place, one, state)


def block_terms(head_input, input_map, output_map, step_size, decay_rate):
    log_decay = -(step_size * decay_rate[None, :]).T
    cumulative = jnp.cumsum(log_decay, axis=1)
    pairwise = cumulative[:, :, None] - cumulative[:, None, :]
    length = cumulative.shape[1]
    causal = jnp.arange(length)[:, None] >= jnp.arange(length)[None, :]
    pair_decay = jnp.exp(jnp.where(causal[None], pairwise, -jnp.inf))
    scores = jnp.dot(output_map, input_map.T, preferred_element_type=jnp.float32)
    mixing = scores[None] * pair_decay * step_size.T[:, None, :]
    inner_out = jnp.einsum("hij,jhp->ihp", mixing, head_input, precision=lax.Precision.HIGH)
    to_end = jnp.exp(cumulative[:, -1:] - cumulative) * step_size.T
    local_state = jnp.einsum(
        "hj,jhp,jn->hpn",
        to_end,
        head_input,
        input_map.astype(jnp.float32),
        precision=lax.Precision.HIGH,
    )
    return (inner_out, cumulative, local_state)


def carried(output_map, cumulative, state):
    reach = jnp.einsum(
        "in,hpn->ihp", output_map.astype(jnp.float32), state, precision=lax.Precision.HIGH
    )
    return jnp.exp(cumulative).T[:, :, None] * reach


def compose(earlier, later):
    return (earlier[0] * later[0], later[0][:, None, None] * earlier[1] + later[1])


def local(
    tokens, bounds, in_weight, conv_weight, conv_bias, dt_bias, decay_rate, skip_gain, norm_gain
):
    slots = tokens.shape[1]
    inner = norm_gain.shape[0]
    state_width = (conv_bias.shape[0] - inner) // 2
    heads = decay_rate.shape[0]
    head_dim = inner // heads
    kernel = conv_weight.shape[0]
    capacity = slots // BLOCK
    shard_blocks = bounds[0, 0, 1] - bounds[0, 0, 0]
    own_rows = tokens[0]
    summed = jnp.dot(
        own_rows,
        lax.all_gather(in_weight, ("seq", "fsdp"), axis=0, tiled=True),
        preferred_element_type=jnp.float32,
    )
    projected = summed.astype(jnp.bfloat16)
    gate = projected[:, :inner].astype(jnp.float32)
    mixed_in = projected[:, inner : 2 * inner + 2 * state_width]
    raw_step = projected[:, 2 * inner + 2 * state_width :].astype(jnp.float32)
    edge_rows = lax.dynamic_slice_in_dim(
        mixed_in, shard_blocks * BLOCK - (kernel - 1), kernel - 1, 0
    )
    previous = passed_along(edge_rows, "seq", 1)
    extended = jnp.concatenate([previous, mixed_in], axis=0)
    convolved = jnp.zeros((slots, mixed_in.shape[1]), jnp.float32) + conv_bias[None, :]
    for offset in range(kernel):
        convolved = convolved + conv_weight[offset][None, :] * extended[
            offset : offset + slots
        ].astype(jnp.float32)
    conv_out = jax.nn.silu(convolved).astype(jnp.bfloat16)
    live_mask = jnp.arange(slots)[:, None] < shard_blocks * BLOCK
    step_size = jnp.where(live_mask, jax.nn.softplus(raw_step + dt_bias[None, :]), 0.0)
    pieces = []
    decay_total = jnp.ones((heads,), jnp.float32)
    summary_state = jnp.zeros((heads, head_dim, state_width), jnp.float32)
    for place in range(capacity):
        lower = place * BLOCK
        upper = lower + BLOCK
        in_values = (
            conv_out[lower:upper, :inner].astype(jnp.float32).reshape(BLOCK, heads, head_dim)
        )
        in_map = conv_out[lower:upper, inner : inner + state_width]
        out_map = conv_out[lower:upper, inner + state_width :]
        inner_out, cumulative, local_state = block_terms(
            in_values, in_map, out_map, step_size[lower:upper], decay_rate
        )
        block_decay = jnp.exp(cumulative[:, -1])
        summary_state = block_decay[:, None, None] * summary_state + local_state
        decay_total = decay_total * block_decay
        pieces.append((in_values, out_map, inner_out, cumulative, local_state, block_decay))
    identity = (
        jnp.ones((heads,), jnp.float32),
        jnp.zeros((heads, head_dim, state_width), jnp.float32),
    )
    incoming = carried_in((decay_total, summary_state), "seq", compose, identity)
    state = incoming[1]
    results = []
    for in_values, out_map, inner_out, cumulative, local_state, block_decay in pieces:
        result = (
            inner_out + carried(out_map, cumulative, state) + skip_gain[None, :, None] * in_values
        )
        results.append(result.reshape(BLOCK, inner))
        state = block_decay[:, None, None] * state + local_state
    scanned = jnp.concatenate(results, axis=0)
    gated = scanned * jax.nn.silu(gate)
    normed = (
        gated
        * lax.rsqrt(jnp.mean(gated * gated, axis=1, keepdims=True) + 1e-05)
        * norm_gain[None, :]
    )
    layer_out = jnp.where(live_mask, normed, 0.0).astype(jnp.bfloat16)
    return layer_out[None]


def solution(mesh):
    in_specs = (
        P("fsdp", "seq", None),
        P("fsdp", "seq", None),
        P(("seq", "fsdp"), None),
        P(),
        P(),
        P(),
        P(),
        P(),
        P(),
    )
    out_specs = P("fsdp", "seq", None)
    return jax.shard_map(local, mesh=mesh, in_specs=in_specs, out_specs=out_specs, check_vma=False)
```

profile of v0, /device:TPU:31, one launch (start us, length us, event | category | flops | bytes accessed | tf_op | source)
XLA Modules:
  0.0 540.5 jit_solution(17595913890075685006)
XLA Ops:
  11.0 166.1 %all-gather.5.cloned.1.call-done = bf16[2560,5416]{1,0:T(8,128)(2,1)} async-done(((bf16[80,5416]{1,0:T(8,128)(2,1)}), bf16[2560,5416]{1,0:T(8,128)(2,1)}) %all-gather.5.cloned.1.call-update) | async-done | bytes 27729936 | tf_op jit(solution)/shard_map/all_gather | solution.py:74
  177.1 28.9 %convolution_convert_fusion = bf16[768,5416]{0,1:T(8,128)(2,1)} fusion(bf16[2560,5416]{1,0:T(8,128)(2,1)} %all-gather.5.cloned.1.call-done, bf16[1,768,2560]{2,1,0:T(8,128)(2,1)} %param.11), kind=kOutput, calls=%fused_computation.20 | convolution fusion | flops 21300738048 | bytes 39981056 | tf_op jit(solution)/shard_map/dot_general | solution.py:72
  206.1 4.5 slice.135
  219.1 2.0 collective-permute-done
  221.6 15.4 %multiply_convert_fusion = bf16[768,2816]{0,1:T(8,128)(2,1)S(1)} fusion(bf16[768,2816]{0,1:T(8,128)(2,1)} %slice.135, bf16[3,2816]{0,1:T(8,128)(2,1)S(1)} %copy.37, f32[2816]{0:T(1024)S(1)} %get-tuple-element.52, f32[2816]{0:T(1024)S(1)} %get-tuple-element.53, f32[2816]{0:T(1024)S(1)} %get-tuple-element.51, f32[2816]{0:T(1024)S(1)} %get-tuple-element.50, ...), kind=kLoop, calls=%fused_computation.23 | loop fusion | flops 56229888 | bytes 8723968 | tf_op jit(solution)/shard_map/convert_element_type | solution.py:91
  240.7 1.9 fusion.56
  244.7 31.0 %all-reduce = f32[640]{0:T(1024)S(1)} all-reduce(f32[640]{0:T(1024)S(1)} %dynamic-update-slice), channel_id=2, replica_groups=mesh['seq'=16,'fsdp'=2] {'seq'}, use_global_device_ids=true, to_apply=%add | all-reduce | flops 640 | bytes 5120
  279.1 194.9 %all-gather.7.cloned.1.call-done = f32[640,64,128]{2,1,0:T(8,128)} async-done(((f32[40,64,128]{2,1,0:T(8,128)}), f32[640,64,128]{2,1,0:T(8,128)}) %all-gather.7.cloned.1.call-update) | async-done | bytes 20971536 | tf_op jit(solution)/shard_map/all_gather | solution.py:17
  474.1 24.6 %while.12 = (s32[]{:T(128)}, f32[40,64,128]{2,1,0:T(8,128)S(1)}, s32[]{:T(128)}, f32[16,40]{1,0:T(8,128)S(1)}, f32[16,40,64,128]{3,2,1,0:T(8,128)}, /*index=5*/s32[]{:T(128)}, s32[]{:T(128)}, s32[]{:T(128)}) while((s32[]{:T(128)}, f32[40,64,128]{2,1,0:T(8,128)S(1)}, s32[]{:T(128)}, f32[16,40]{1,0:T(8,128)S(1)}, f32[16,40,64,128]{3,2,1,0:T(8,128)}, ...), condition=%wide.region_7.8_spmd, body=%wide.region_6.7_spmd.sunk | while | flops 655365 | bytes 3932767 | solution.py:25
  474.1 1.6 bitcast_add_fusion.5
  475.8 1.6 bitcast_add_fusion.5
  477.4 1.6 bitcast_add_fusion.5
  479.0 1.6 bitcast_add_fusion.5
  480.6 1.6 bitcast_add_fusion.5
  482.3 1.6 bitcast_add_fusion.5
  483.9 1.6 bitcast_add_fusion.5
  485.5 1.6 bitcast_add_fusion.5
  487.2 1.6 bitcast_add_fusion.5
  488.8 1.6 bitcast_add_fusion.5
  490.4 1.6 bitcast_add_fusion.5
  492.0 1.6 bitcast_add_fusion.5
  493.7 1.6 bitcast_add_fusion.5
  495.3 1.6 bitcast_add_fusion.5
  498.7 1.8 fusion.71
  500.5 1.7 fusion.64
  502.3 1.8 fusion.57
  504.2 5.2 fusion.45
  509.5 5.5 %fusion.47 = f32[256,40,64]{0,2,1:T(8,128)S(1)} fusion(bf16[256,40,64]{0,2,1:T(8,128)(2,1)S(1)} %bitcast.128, f32[256,40,64]{0,2,1:T(8,128)S(1)} %fusion.64, f32[40,256]{1,0:T(8,128)S(1)} %copy-done.14, f32[40,256]{1,0:T(8,128)S(1)} %copy_bitcast_fusion.1, f32[256,256]{1,0:T(8,128)S(1)} %fusion.77, pred[256,256]{1,0:T(8,128)(4,1)S(1)} %copy-done.9, ...), kind=kOutput, calls=%fused_computation.66 | convolution fusion | flops 1020395520 | bytes 7004320 | tf_op jit(solution)/shard_map/hij,jhp->ihp/dot_general | solution.py:37
  515.0 5.2 fusion.49
  520.2 4.4 multiply_reduce_fusion
  524.7 2.6 fusion.42
  527.3 6.3 %copy.50 = bf16[1,768,2560]{2,1,0:T(8,128)(2,1)} copy(bf16[1,768,2560]{1,2,0:T(8,128)(2,1)} %fusion.42) | data formatting | bytes 7864320 | tf_op jit(solution)/shard_map/broadcast_in_dim | solution.py:133
  (108 shorter events, 22.4 us)
Async XLA Ops:
  6.5 170.6 %all-gather.5.cloned.1.call-start = ((), (), s32[]{:S(2)}) async-start(), calls=%async_computation | async-start | bytes 29061120 | tf_op jit(solution)/shard_map/all_gather | solution.py:74
  7.3 466.7 %all-gather.7.cloned.1.call-start = ((), (), s32[]{:S(2)}) async-start(), calls=%async_computation.1 | async-start | bytes 22282240 | tf_op jit(solution)/shard_map/all_gather | solution.py:17
  206.0 4.5 copy-start.18
  206.1 5.5 %copy-start.19 = (f32[40]{0:T(128)S(1)}, f32[40]{0:T(128)}, u32[]{:S(2)}) copy-start(f32[40]{0:T(128)} %param.17) | copy-start | bytes 484
  210.6 11.0 %copy-start.16 = (f32[2816]{0:T(1024)S(1)}, f32[2816]{0:T(1024)}, u32[]{:S(2)}) copy-start(f32[2816]{0:T(1024)} %param.15) | copy-start | bytes 33796
  216.6 4.5 collective-permute-start
  237.0 2.9 copy-start
  237.3 1.4 copy-start.3
  237.3 2.3 copy-start.5
  237.3 3.0 copy-start.7
  239.6 1.1 copy-start.1
  239.6 3.1 copy-start.21
  498.7 3.5 copy-start.2
  502.3 1.9 copy-start.6
  502.3 1.9 copy-start.9
  502.3 1.9 copy-start.12
  502.3 1.9 copy-start.15
  502.3 1.9 copy-start.20
  504.2 5.3 copy-start.4
  504.2 5.2 copy-start.11
  504.2 5.2 copy-start.14
  509.5 5.5 %copy-start.8 = (bf16[256,2560]{0,1:T(8,128)(2,1)S(1)}, bf16[256,2560]{0,1:T(8,128)(2,1)}, u32[]{:S(2)}) copy-start(bf16[256,2560]{0,1:T(8,128)(2,1)} %copy-done.7) | copy-start | bytes 3932164
  509.5 5.5 %copy-start.10 = (f32[256,40]{0,1:T(8,128)S(1)}, f32[256,40]{0,1:T(8,128)}, u32[]{:S(2)}) copy-start(f32[256,40]{0,1:T(8,128)} %get-tuple-element.87) | copy-start | bytes 122884
  509.5 5.5 %copy-start.13 = (f32[40,256]{1,0:T(8,128)S(1)}, f32[40,256]{1,0:T(8,128)}, u32[]{:S(2)}) copy-start(f32[40,256]{1,0:T(8,128)} %get-tuple-element.78) | copy-start | bytes 122884
  520.2 4.5 copy-start.17
Sparse Core Ops, SparseCore 0:
  10.2 166.9 all-gather.4
  242.8 231.1 all-gather.6
where the time goes:
time: 542 us; the launch traced here: 540 us
  waiting for transfers between devices  364 us (67%)
  matrix products  57 us (11%)
  other arithmetic  51.6 us (10%)
  blocking collectives  31 us (6%)
  local copies, waits for them, and re-layouts  18.9 us (3%)
  between operations  15.7 us (3%)
    all_gather x1, waiting for transfers between devices, carried_in(): gathered = jax.tree.map(lambda a: lax.all_gather(a, axis), part)  195 us
    all_gather x1, waiting for transfers between devices, local(): lax.all_gather(in_weight, ('seq', 'fsdp'), axis=0, tiled=True)  166 us
    unnamed x1, blocking collectives  31 us
    dot_general x1, matrix products, local(): jnp.dot(own_rows, lax.all_gather(in_weight, ('seq', 'fsdp'), axis=0, tile...  28.9 us
    add x15, other arithmetic, compose(): later[0][:, None, None] * earlier[1] + later[1]  23.7 us
    dot_general x3, matrix products, block_terms(): jnp.einsum('hij,jhp->ihp', mixing, head_input, precision=lax.Precision.HIGH)  15.9 us
    convert_element_type x1, other arithmetic, local(): conv_out = jax.nn.silu(convolved).astype(jnp.bfloat16)  15.4 us
  transfers between devices with their start and end apart: 3, of which 3 were waited for; matrix products, arithmetic and copies ran while one was open for 2% of the time, Pallas kernels for 0%

commit v1 on v0

--- a/solution.py
+++ b/solution.py
@@ -1,6 +1,7 @@
 import jax
 import jax.numpy as jnp
 from jax import lax
+from jax.experimental import pallas as pl
 from jax.sharding import PartitionSpec as P
 
 BLOCK = 256
@@ -12,17 +13,32 @@
     return lax.ppermute(value, axis, [(source, source + steps) for source in range(leading, last)])
 
 
-def carried_in(part, axis, combine, identity):
-    place = lax.axis_index(axis)
-    gathered = jax.tree.map(lambda a: lax.all_gather(a, axis), part)
-    state = jax.tree.map(lambda a, e: jnp.zeros_like(a) + jnp.asarray(e, a.dtype), part, identity)
+def compose_kernel(state_ref, decay_ref, before_ref):
+    def one(turn, state):
+        before_ref[turn] = state
+        return decay_ref[turn] * state + state_ref[turn]
 
-    def one(turn, state):
-        return combine(
-            state, jax.tree.map(lambda a: lax.dynamic_index_in_dim(a, turn, 0, False), gathered)
-        )
+    lax.fori_loop(0, state_ref.shape[0], one, jnp.zeros(state_ref.shape[1:], jnp.float32))
 
-    return lax.fori_loop(0, place, one, state)
+
+def carried_in(decay_total, summary_state, axis):
+    count = lax.axis_size(axis)
+    heads, head_dim, width = summary_state.shape
+    share = heads * head_dim // count
+    extra = -(-share // width)
+    decay_rows = jnp.repeat(decay_total, head_dim).reshape(count, share)
+    decay_rows = jnp.pad(decay_rows, ((0, 0), (0, extra * width - share)))
+    sent = jnp.concatenate(
+        [summary_state.reshape(count, share, width), decay_rows.reshape(count, extra, width)], axis=1
+    )
+    got = lax.all_to_all(sent, axis, 0, 0)
+    decays = got[:, share:].reshape(count, extra * width)[:, :share, None]
+    before = pl.pallas_call(
+        compose_kernel,
+        out_shape=jax.ShapeDtypeStruct((count, share, width), jnp.float32),
+        cost_estimate=pl.CostEstimate(flops=1000000, bytes_accessed=4000000, transcendentals=0),
+    )(got[:, :share], decays)
+    return lax.all_to_all(before, axis, 0, 0).reshape(heads, head_dim, width)
 
 
 def block_terms(head_input, input_map, output_map, step_size, decay_rate):
@@ -53,10 +69,6 @@
     return jnp.exp(cumulative).T[:, :, None] * reach
 
 
-def compose(earlier, later):
-    return (earlier[0] * later[0], later[0][:, None, None] * earlier[1] + later[1])
-
-
 def local(
     tokens, bounds, in_weight, conv_weight, conv_bias, dt_bias, decay_rate, skip_gain, norm_gain
 ):
@@ -69,15 +81,15 @@
     capacity = slots // BLOCK
     shard_blocks = bounds[0, 0, 1] - bounds[0, 0, 0]
     own_rows = tokens[0]
-    summed = jnp.dot(
-        own_rows,
-        lax.all_gather(in_weight, ("seq", "fsdp"), axis=0, tiled=True),
-        preferred_element_type=jnp.float32,
+    every = ("seq", "fsdp")
+    mixed_weight = lax.all_gather(in_weight[:, inner:], every, axis=0, tiled=True)
+    gate_share, mixed_weight = lax.optimization_barrier((in_weight[:, :inner], mixed_weight))
+    gate_weight = lax.all_gather(gate_share, every, axis=0, tiled=True)
+    projected = jnp.dot(own_rows, mixed_weight, preferred_element_type=jnp.float32).astype(
+        jnp.bfloat16
     )
-    projected = summed.astype(jnp.bfloat16)
-    gate = projected[:, :inner].astype(jnp.float32)
-    mixed_in = projected[:, inner : 2 * inner + 2 * state_width]
-    raw_step = projected[:, 2 * inner + 2 * state_width :].astype(jnp.float32)
+    mixed_in = projected[:, : inner + 2 * state_width]
+    raw_step = projected[:, inner + 2 * state_width :].astype(jnp.float32)
     edge_rows = lax.dynamic_slice_in_dim(
         mixed_in, shard_blocks * BLOCK - (kernel - 1), kernel - 1, 0
     )
@@ -109,12 +121,10 @@
         summary_state = block_decay[:, None, None] * summary_state + local_state
         decay_total = decay_total * block_decay
         pieces.append((in_values, out_map, inner_out, cumulative, local_state, block_decay))
-    identity = (
-        jnp.ones((heads,), jnp.float32),
-        jnp.zeros((heads, head_dim, state_width), jnp.float32),
+    state = carried_in(decay_total, summary_state, "seq")
+    gate = lax.reduce_precision(
+        jnp.dot(own_rows, gate_weight, preferred_element_type=jnp.float32), 8, 7
     )
-    incoming = carried_in((decay_total, summary_state), "seq", compose, identity)
-    state = incoming[1]
     results = []
     for in_values, out_map, inner_out, cumulative, local_state, block_decay in pieces:
         result = (

time: 542 us -> 346 us (0.64)
  waiting for transfers between devices: 364 us -> 131 us
  blocking collectives: 31 us -> 69.6 us
  other arithmetic: 51.6 us -> 25.1 us
  matrix products: 57 us -> 65.7 us
  starting transfers between devices: 1.51 us -> 8.27 us
    all_gather x2, waiting for transfers between devices: 361 us -> 105 us  [the longest x1 105 us: local(): lax.all_gather(in_weight[:, inner:], every, axis=0, tiled=True)]
    all_to_all x0 -> x1, blocking collectives: none -> 69.6 us  [carried_in(): got = lax.all_to_all(sent, axis, 0, 0)]
    unnamed x1 -> x0, blocking collectives: 31 us -> none
    all_to_all x0 -> x1, waiting for transfers between devices: none -> 23.9 us  [carried_in(): return lax.all_to_all(before, axis, 0, 0).reshape(heads, head_dim, width)]
    add x15 -> x0, other arithmetic: 23.7 us -> none  [compose(): later[0][:, None, None] * earlier[1] + later[1]]
    dot_general x1 -> x2, matrix products: 28.9 us -> 36 us  [the longest x1 19.3 us: local(): jnp.dot(own_rows, gate_weight, preferred_element_type=jnp.float32)]
    all_to_all x0 -> x1, starting transfers between devices: none -> 6.94 us  [carried_in(): return lax.all_to_all(before, axis, 0, 0).reshape(heads, head_dim, width)]
  transfers between devices with their start and end apart: 3 -> 4, of which waited for: 3 -> 3; matrix products, arithmetic and copies ran while one was open for 2% -> 23% of each run, Pallas kernels for 0% -> 1%
where the time goes in v1:
time: 346 us; the launch traced here: 340 us
  waiting for transfers between devices  131 us (38%)
  blocking collectives  69.6 us (20%)
  matrix products  65.7 us (19%)
  other arithmetic  25.1 us (7%)
  local copies, waits for them, and re-layouts  21.6 us (6%)
  between operations  15.1 us (4%)
  starting transfers between devices  8.27 us (2%)
  Pallas kernels  4.44 us (1%)
    all_gather x1, waiting for transfers between devices, local(): lax.all_gather(in_weight[:, inner:], every, axis=0, tiled=True)  105 us
    all_to_all x1, blocking collectives, carried_in(): got = lax.all_to_all(sent, axis, 0, 0)  69.6 us
    all_to_all x1, waiting for transfers between devices, carried_in(): return lax.all_to_all(before, axis, 0, 0).reshape(heads, head_dim, width)  23.9 us
    dot_general x1, matrix products, local(): jnp.dot(own_rows, gate_weight, preferred_element_type=jnp.float32)  19.3 us
    dot_general x3, matrix products, block_terms(): jnp.einsum('hij,jhp->ihp', mixing, head_input, precision=lax.Precision.HIGH)  18.7 us
    dot_general x1, matrix products, local(): jnp.dot(own_rows, mixed_weight, preferred_element_type=jnp.float32)  16.6 us
    convert_element_type x1, other arithmetic, local(): conv_out = jax.nn.silu(convolved).astype(jnp.bfloat16)  15.4 us
    all_to_all x1, starting transfers between devices, carried_in(): return lax.all_to_all(before, axis, 0, 0).reshape(heads, head_dim, width)  6.94 us
  transfers between devices with their start and end apart: 4, of which 3 were waited for; matrix products, arithmetic and copies ran while one was open for 23% of the time, Pallas kernels for 1%

profile of v1, /device:TPU:31, one launch (start us, length us, event | category | flops | bytes accessed | tf_op | source)
XLA Modules:
  0.0 340.5 jit_solution(6312523808577222663)
XLA Ops:
  6.5 1.8 slice.118
  8.4 1.8 slice.117
  10.2 105.1 %all-gather.3.cloned.1.call-done = bf16[2560,2856]{1,0:T(8,128)(2,1)} async-done(((bf16[80,2856]{1,0:T(8,128)(2,1)}), bf16[2560,2856]{1,0:T(8,128)(2,1)}) %all-gather.3.cloned.1.call-update) | async-done | bytes 14622736 | tf_op jit(solution)/shard_map/all_gather | solution.py:85
  115.4 1.4 fusion.94
  118.1 1.1 slice_reduce_fusion.9
  119.1 16.6 %fusion.39 = bf16[768,2856]{0,1:T(8,128)(2,1)S(1)} fusion(bf16[2560,2856]{1,0:T(8,128)(2,1)} %all-gather.3.cloned.1.call-done, bf16[1,768,2560]{2,1,0:T(8,128)(2,1)} %param.9), kind=kOutput, calls=%fused_computation.50 | convolution fusion | flops 11232442368 | bytes 22941696 | tf_op jit(solution)/shard_map/dot_general | solution.py:88
  135.8 2.3 slice.151
  141.3 1.4 constant_dynamic-slice_fusion
  143.0 1.3 collective-permute-start
  146.0 1.5 collective-permute-done
  147.9 15.4 %multiply_convert_fusion = bf16[768,2816]{0,1:T(8,128)(2,1)S(1)} fusion(bf16[768,2816]{0,1:T(8,128)(2,1)} %slice.151, bf16[3,2816]{0,1:T(8,128)(2,1)S(1)} %copy.38, f32[2816]{0:T(1024)S(1)} %get-tuple-element.11, f32[2816]{0:T(1024)S(1)} %get-tuple-element.12, f32[2816]{0:T(1024)S(1)} %get-tuple-element.10, f32[2816]{0:T(1024)S(1)} %get-tuple-element.9, ...), kind=kLoop, calls=%fused_computation.18 | loop fusion | flops 56229888 | bytes 8723968 | tf_op jit(solution)/shard_map/convert_element_type | solution.py:103
  163.7 0.9 fusion.45
  164.5 0.8 fusion.47
  165.4 0.9 fusion.57
  167.0 69.6 %all_to_all.10 = f32[16,162,128]{2,1,0:T(8,128)S(1)} all-to-all(f32[16,162,128]{2,1,0:T(8,128)S(1)} %pad_maximum_fusion.1), channel_id=1, replica_groups=mesh['seq'=16,'fsdp'=2] {'seq'}, dimensions={0} | all-to-all | bytes 2654208 | tf_op jit(solution)/shard_map/all_to_all | solution.py:34
  236.7 1.5 copy.48.decay_ref
  238.2 1.2 slice.173.state_ref
  239.4 4.4 %shard_map.91 = f32[16,160,128]{2,1,0:T(8,128)} custom-call(f32[16,160,128]{2,1,0:T(8,128)} %slice.173.state_ref, f32[16,160,1]{2,1,0:T(8,128)} %copy.48.decay_ref), custom_call_target="tpu_custom_call" | custom-call | flops 1000000 | bytes 4000000 | tf_op jit(solution)/shard_map/pallas_call | solution.py:36
  243.9 6.9 %all-to-all-start.1 = ((f32[16,160,128]{2,1,0:T(8,128)}), f32[16,160,128]{2,1,0:T(8,128)S(1)}, u32[]{:S(2)}, u32[]{:S(2)}) async-start(f32[16,160,128]{2,1,0:T(8,128)} %shard_map.91), calls=%async_computation.1 | async-start | bytes 2621440 | tf_op jit(solution)/shard_map/all_to_all | solution.py:41
  251.4 1.1 fusion.85
  252.5 1.1 fusion.78
  253.6 1.1 fusion.75
  254.7 23.9 %all-to-all-done.1 = f32[16,160,128]{2,1,0:T(8,128)S(1)} async-done(((f32[16,160,128]{2,1,0:T(8,128)}), f32[16,160,128]{2,1,0:T(8,128)S(1)}, u32[]{:S(2)}, u32[]{:S(2)}) %all-to-all-start.1) | async-done | bytes 1310752 | tf_op jit(solution)/shard_map/all_to_all | solution.py:41
  278.6 1.8 fusion.72
  280.3 1.7 fusion.65
  282.1 1.8 fusion.58
  284.1 5.2 %fusion.46 = f32[256,40,64]{0,2,1:T(8,128)S(1)} fusion(bf16[256,40,64]{0,2,1:T(8,128)(2,1)S(1)} %bitcast.152, f32[256,40,64]{0,2,1:T(8,128)S(1)} %fusion.72, f32[40,256]{1,0:T(8,128)S(1)} %copy-done.15, f32[40,256]{1,0:T(8,128)S(1)} %copy_bitcast_fusion.2, f32[256,256]{1,0:T(8,128)S(1)} %fusion.85, pred[256,256]{1,0:T(8,128)(4,1)S(1)} %copy-done.9, ...), kind=kOutput, calls=%fused_computation.64 | convolution fusion | flops 1020395520 | bytes 7004320 | tf_op jit(solution)/shard_map/hij,jhp->ihp/dot_general | solution.py:53
  289.3 6.7 %fusion.48 = f32[256,40,64]{0,2,1:T(8,128)} fusion(bf16[256,40,64]{0,2,1:T(8,128)(2,1)S(1)} %bitcast.150, f32[256,40,64]{0,2,1:T(8,128)S(1)} %fusion.65, f32[40,256]{1,0:T(8,128)S(1)} %copy-done.14, f32[40,256]{1,0:T(8,128)S(1)} %copy_bitcast_fusion, f32[256,256]{1,0:T(8,128)S(1)} %fusion.78, pred[256,256]{1,0:T(8,128)(4,1)S(1)} %copy-done.9, ...), kind=kOutput, calls=%fused_computation.66 | convolution fusion | flops 1020395520 | bytes 7004320 | tf_op jit(solution)/shard_map/hij,jhp->ihp/dot_general | solution.py:53
  296.1 6.7 %fusion.50 = f32[256,40,64]{0,2,1:T(8,128)} fusion(bf16[256,40,64]{0,2,1:T(8,128)(2,1)S(1)} %bitcast.154, f32[256,40,64]{0,2,1:T(8,128)S(1)} %fusion.58, f32[40,256]{1,0:T(8,128)S(1)} %copy-done.13, f32[40,256]{1,0:T(8,128)S(1)} %copy_bitcast_fusion.1, f32[256,256]{1,0:T(8,128)S(1)} %fusion.75, pred[256,256]{1,0:T(8,128)(4,1)S(1)} %copy-done.9, ...), kind=kOutput, calls=%fused_computation.68 | convolution fusion | flops 1020395520 | bytes 7004320 | tf_op jit(solution)/shard_map/hij,jhp->ihp/dot_general | solution.py:53
  302.8 19.3 %multiply_reduce_fusion = (f32[768]{0:T(1024)S(1)}, f32[768,2560]{0,1:T(8,128)}) fusion(bf16[2560,2560]{1,0:T(8,128)(2,1)} %all-gather.5.cloned.1.call-done, bf16[1,768,2560]{2,1,0:T(8,128)(2,1)} %param.9, f32[256,2560]{0,1:T(8,128)} %bitcast.160, f32[256,2560]{0,1:T(8,128)} %bitcast.159, f32[256,2560]{0,1:T(8,128)S(1)} %bitcast.158), kind=kOutput, calls=%fused_computation.26 | convolution fusion | flops 10085989376 | bytes 32771072 | tf_op jit(solution)/shard_map/dot_general | solution.py:126
  322.1 5.2 %fusion.42 = bf16[1,768,2560]{1,2,0:T(8,128)(2,1)} fusion(f32[768,2560]{0,1:T(8,128)} %get-tuple-element.39, f32[2560]{0:T(1024)S(1)} %copy-done.17, f32[768]{0:T(1024)S(1)} %add_rsqrt_fusion, pred[768]{0:T(1024)(128)(4,1)S(1)} %iota_compare_fusion.1), kind=kLoop, calls=%fused_computation.54 | loop fusion | flops 7864320 | bytes 11810560 | tf_op jit(solution)/shard_map/broadcast_in_dim | solution.py:143
  327.4 6.3 %copy.52 = bf16[1,768,2560]{2,1,0:T(8,128)(2,1)} copy(bf16[1,768,2560]{1,2,0:T(8,128)(2,1)} %fusion.42) | data formatting | bytes 7864320 | tf_op jit(solution)/shard_map/broadcast_in_dim | solution.py:143
  (85 shorter events, 7.4 us)
Async XLA Ops:
  6.5 108.8 %all-gather.3.cloned.1.call-start = ((), (), s32[]{:S(2)}) async-start(), calls=%async_computation.2 | async-start | bytes 15544320 | tf_op jit(solution)/shard_map/all_gather | solution.py:85
  8.4 294.4 %all-gather.5.cloned.1.call-start = ((), (), s32[]{:S(2)}) async-start(), calls=%async_computation.3 | async-start | bytes 13516800 | tf_op jit(solution)/shard_map/all_gather | solution.py:87
  135.8 2.3 copy-start.18
  135.8 2.4 copy-start.19
  138.1 9.9 %copy-start.16 = (f32[2816]{0:T(1024)S(1)}, f32[2816]{0:T(1024)}, u32[]{:S(2)}) copy-start(f32[2816]{0:T(1024)} %param.13) | copy-start | bytes 33796
  143.0 4.5 %collective-permute-start = (bf16[3,2816]{1,0:T(4,128)(2,1)S(1)}, bf16[3,2816]{1,0:T(4,128)(2,1)S(1)}, u32[]{:S(2)}, u32[]{:S(2)}) collective-permute-start(bf16[3,2816]{1,0:T(4,128)(2,1)S(1)} %copy.37), channel_id=1, source_target_pairs={{0,2},{2,4},{4,6},{6,8},{8,10},{10,12},{12,14},{14,16},{16,18},{18... | collective-permute-start | bytes 50696 | tf_op jit(solution)/shard_map/ppermute | solution.py:13
  163.4 2.0 copy-start
  163.6 2.6 copy-start.3
  163.7 2.6 copy-start.5
  163.7 3.0 copy-start.7
  165.4 1.6 copy-start.1
  243.9 34.7 %all-to-all-start.1 = ((f32[16,160,128]{2,1,0:T(8,128)}), f32[16,160,128]{2,1,0:T(8,128)S(1)}, u32[]{:S(2)}, u32[]{:S(2)}) async-start(f32[16,160,128]{2,1,0:T(8,128)} %shard_map.91), calls=%async_computation.1 | async-start | bytes 2621440 | tf_op jit(solution)/shard_map/all_to_all | solution.py:41
  278.6 3.5 %copy-start.2 = (f32[40,64,128]{2,1,0:T(8,128)S(1)}, f32[40,64,128]{2,1,0:T(8,128)}, u32[]{:S(2)}) copy-start(f32[40,64,128]{2,1,0:T(8,128)} %copy-done.1) | copy-start | bytes 3932164
  282.1 1.9 copy-start.6
  282.1 1.9 copy-start.9
  282.1 1.9 copy-start.12
  282.1 1.9 copy-start.15
  282.1 1.9 copy-start.20
  284.0 5.2 %copy-start.4 = (bf16[256,2560]{0,1:T(8,128)(2,1)S(1)}, bf16[256,2560]{0,1:T(8,128)(2,1)}, u32[]{:S(2)}) copy-start(bf16[256,2560]{0,1:T(8,128)(2,1)} %copy-done.3) | copy-start | bytes 3932164
  284.0 5.2 %copy-start.11 = (f32[256,40]{0,1:T(8,128)S(1)}, f32[256,40]{0,1:T(8,128)}, u32[]{:S(2)}) copy-start(f32[256,40]{0,1:T(8,128)} %get-tuple-element.29) | copy-start | bytes 122884
  284.1 5.2 %copy-start.14 = (f32[40,256]{1,0:T(8,128)S(1)}, f32[40,256]{1,0:T(8,128)}, u32[]{:S(2)}) copy-start(f32[40,256]{1,0:T(8,128)} %get-tuple-element.21) | copy-start | bytes 122884
  289.3 6.8 %copy-start.8 = (bf16[256,2560]{0,1:T(8,128)(2,1)S(1)}, bf16[256,2560]{0,1:T(8,128)(2,1)}, u32[]{:S(2)}) copy-start(bf16[256,2560]{0,1:T(8,128)(2,1)} %copy-done.7) | copy-start | bytes 3932164
  289.3 6.8 %copy-start.10 = (f32[256,40]{0,1:T(8,128)S(1)}, f32[256,40]{0,1:T(8,128)}, u32[]{:S(2)}) copy-start(f32[256,40]{0,1:T(8,128)} %get-tuple-element.30) | copy-start | bytes 122884
  289.3 6.8 %copy-start.13 = (f32[40,256]{1,0:T(8,128)S(1)}, f32[40,256]{1,0:T(8,128)}, u32[]{:S(2)}) copy-start(f32[40,256]{1,0:T(8,128)} %get-tuple-element.20) | copy-start | bytes 122884
  302.8 19.3 %copy-start.17 = (f32[2560]{0:T(1024)S(1)}, f32[2560]{0:T(1024)}, u32[]{:S(2)}) copy-start(f32[2560]{0:T(1024)} %param.17) | copy-start | bytes 30724
Sparse Core Ops, SparseCore 0:
  10.2 105.1 all-gather.2
  118.2 124.8 all-gather.4
